TPU v7x, 32 devices: a whole 2x2x4 slice. The times are simulated.
32 devices in a mesh: expert: 16 (over z, y, x), width: 2 (over core).
Axes of the slice: x: 2, y: 2, z: 4, core: 2. Of those that a mesh axis runs over, the one named last changes fastest.
Arguments:
- tokens: bfloat16 [1024, 6144], P('expert', 'width'), may hold values from -6 to 6
- expert_ids: int32 [1024, 8], P('expert'), may hold values from 0 to 383, all different within a row; in each aligned block of 64 rows (0 to 63, 64 to 127, ...) at most 2 rows name the same one
- route_weight: float32 [1024, 8], P('expert'), may hold values from 0.2 to 1.5
- gate_weight: bfloat16 [16, 6144, 1024], P('expert', None, 'width'), may hold values from -0.078125 to 0.078125
- up_weight: bfloat16 [16, 6144, 1024], P('expert', None, 'width'), may hold values from -0.078125 to 0.078125
- down_weight: bfloat16 [16, 6144, 1024], P('expert', None, 'width'), may hold values from -0.1875 to 0.1875
Outputs:
- mixed: bfloat16 [1024, 6144], P('expert', 'width')
Inputs may be any that keep to these rules, and one draw needn't show every extreme that they name: `expert_ids`: each row names 8 different experts. In each aligned block of 64 rows (the rows of one index of the expert axis) no expert is named by more than 2 rows.
All inputs are finite; a program needn't handle non-finite values.
Results may differ from a plain program's by a relative error of at most 0.014.
Values may be sent and summed in bfloat16 or wider, within the bound.
No kernel may reach another device: no remote copies, remote signals or barrier semaphores. Data moves between devices by JAX's collectives and lax.ppermute only.
A program may use at most 64 MiB of HBM per device.

v0:
```python
import jax
import jax.numpy as jnp
from jax import lax
from jax.sharding import PartitionSpec as P

SEND = 2


def local_slots(route_ids, holders):
    experts_held = jnp.arange(holders, dtype=jnp.int32)
    route_hits = route_ids[:, :, None] == experts_held[None, None, :]
    matched = jnp.any(route_hits, axis=1).astype(jnp.int32)
    ranking = jnp.cumsum(matched, axis=0) - matched
    return (route_hits, matched, ranking)


def body(tokens, expert_ids, route_weight, gate_weight, up_weight, down_weight):
    holders = lax.axis_size("expert")
    tok_rows = tokens.shape[0]
    capacity = holders * SEND
    route_hits, matched, ranking = local_slots(expert_ids, holders)
    expert_base = jnp.arange(holders, dtype=jnp.int32)[None, :] * SEND
    slot_of = jnp.where(matched > 0, expert_base + ranking, capacity)
    row_number = jnp.broadcast_to(jnp.arange(tok_rows, dtype=jnp.int32)[:, None], slot_of.shape)
    slot_table = (
        jnp.full((capacity + 1,), tok_rows, jnp.int32)
        .at[slot_of.reshape(-1)]
        .set(row_number.reshape(-1))
    )
    outgoing = jnp.take(tokens, slot_table[:capacity], axis=0, mode="fill", fill_value=0)
    arrived = lax.all_to_all(
        outgoing.reshape(holders, SEND, outgoing.shape[1]),
        "expert",
        split_axis=0,
        concat_axis=0,
        tiled=True,
    )
    selected = arrived.reshape(capacity, arrived.shape[2])
    gate_mat = gate_weight[0]
    up_mat = up_weight[0]
    down_mat = down_weight[0]
    segment = lax.all_gather(selected, "width", axis=1, tiled=True)
    gate_val = jnp.dot(segment, gate_mat, preferred_element_type=jnp.float32)
    up_val = jnp.dot(segment, up_mat, preferred_element_type=jnp.float32)
    hidden = (jax.nn.silu(gate_val) * up_val).astype(jnp.bfloat16)
    weights_held = jnp.sum(jnp.where(route_hits, route_weight[:, :, None], 0.0), axis=1)
    slot_onehot = (ranking[:, :, None] == jnp.arange(SEND, dtype=jnp.int32)[None, None, :]) & (
        matched[:, :, None] > 0
    )
    coeff = (weights_held[:, :, None] * slot_onehot.astype(jnp.float32)).reshape(tok_rows, capacity)
    feature_rows = down_mat.shape[0] // lax.axis_size("width")
    summed = lax.psum_scatter(
        lax.dot_general(
            down_mat, hidden, (((1,), (1,)), ((), ())), preferred_element_type=jnp.float32
        ).astype(jnp.bfloat16),
        "width",
        scatter_dimension=0,
        tiled=True,
    ).astype(jnp.float32)
    returned = lax.all_to_all(
        summed.reshape(feature_rows, holders, SEND).astype(jnp.bfloat16),
        "expert",
        split_axis=1,
        concat_axis=1,
        tiled=True,
    ).astype(jnp.float32)
    returned = returned.reshape(feature_rows, capacity)
    combined = lax.dot_general(
        coeff,
        returned,
        (((1,), (1,)), ((), ())),
        precision=lax.Precision.HIGHEST,
        preferred_element_type=jnp.float32,
    )
    return combined.astype(jnp.bfloat16)


def solution(mesh):
    in_specs = (
        P("expert", "width"),
        P("expert", None),
        P("expert", None),
        P("expert", None, "width"),
        P("expert", None, "width"),
        P("expert", None, "width"),
    )
    out_specs = P("expert", "width")
    return jax.shard_map(body, mesh=mesh, in_specs=in_specs, out_specs=out_specs, check_vma=False)
```

profile of v0, /device:TPU:0, one launch (start us, length us, event | category | flops | bytes accessed | tf_op | source)
XLA Modules:
  0.0 75.9 jit_solution(6627106244274575018)
XLA Ops:
  6.5 0.0 copy-start
  6.5 0.0 reduce-scatter.2.cloned.1.call-start
  6.5 0.8 fusion.21
  7.3 0.1 copy.22
  7.4 0.1 reshape.111
  7.5 0.1 reduce_window_sum.11
  7.6 0.1 select_n.44
  7.7 4.3 %scatter_custom_fusion = s32[33]{0:T(128)S(1)} fusion(s32[1024]{0:T(1024)S(1)} %bitcast.27, s32[1024]{0:T(1024)S(1)} %reshape.111, s32[]{:T(128)} %constant.14.clone.1), kind=kCustom, calls=%fused_computation.40 | custom fusion | bytes 136 | tf_op jit(solution)/shard_map/scatter | solution.py:28
  12.0 0.1 slice.6
  12.1 0.0 copy-done
  12.2 0.7 gather_fusion
  12.8 0.1 gather.7
  12.9 0.3 broadcast_select_fusion
  13.2 16.8 %all_to_all.10 = bf16[16,2,3072]{2,1,0:T(2,128)(2,1)S(1)} all-to-all(bf16[16,2,3072]{2,1,0:T(2,128)(2,1)S(1)} %broadcast_select_fusion), channel_id=1, replica_groups=mesh['expert'=16,'width'=2] {'expert'}, dimensions={0} | all-to-all | bytes 393216 | tf_op jit(solution)/shard_map/all_to_all | solution.py:31
  30.0 0.1 reshape.98
  30.0 2.1 %all_gather.3 = bf16[32,6144]{1,0:T(8,128)(2,1)S(1)} all-gather(bf16[32,3072]{1,0:T(8,128)(2,1)S(1)} %reshape.98), channel_id=1, replica_groups=mesh['expert'=16,'width'=2] {'width'}, dimensions={1}, use_global_device_ids=true | all-gather | bytes 589824 | tf_op jit(solution)/shard_map/all_gather | solution.py:42
  32.1 3.9 %fusion.4 = f32[32,512]{1,0:T(8,128)S(1)} fusion(bf16[32,6144]{1,0:T(8,128)(2,1)S(1)} %all_gather.3, bf16[1,6144,512]{2,1,0:T(8,128)(2,1)} %param.9), kind=kOutput, calls=%fused_computation.7 | convolution fusion | flops 201326592 | bytes 6750208 | tf_op jit(solution)/shard_map/dot_general | solution.py:43
  36.1 0.0 copy-start.1
  36.1 0.0 copy-start.2
  36.1 8.4 %fusion = bf16[6144,32]{0,1:T(8,128)(2,1)} fusion(bf16[1,6144,512]{2,1,0:T(8,128)(2,1)} %param.11, bf16[32,6144]{1,0:T(8,128)(2,1)S(1)} %all_gather.3, bf16[1,6144,512]{2,1,0:T(8,128)(2,1)} %param.10, f32[32,512]{1,0:T(8,128)S(1)} %fusion.4), kind=kOutput, calls=%fused_computation.3 | convolution fusion | flops 402948096 | bytes 13434880 | tf_op jit(solution)/shard_map/dot_general | solution.py:53
  44.5 0.0 reduce-scatter.2.cloned.1.call-update
  44.5 5.7 %reduce-scatter.2.cloned.1.call-done = bf16[3072,32]{0,1:T(8,128)(2,1)} async-done(((bf16[6144,32]{0,1:T(8,128)(2,1)}), bf16[3072,32]{0,1:T(8,128)(2,1)}) %reduce-scatter.2.cloned.1.call-update) | async-done | bytes 196624 | tf_op jit(solution)/shard_map/reduce_scatter | solution.py:52
  50.2 1.7 %convert_element_type.42 = bf16[3072,16,2]{0,2,1:T(2,128)(2,1)} reshape(bf16[3072,32]{0,1:T(8,128)(2,1)} %reduce-scatter.2.cloned.1.call-done) | data formatting | bytes 393216 | tf_op jit(solution)/shard_map/convert_element_type | solution.py:61
  51.9 6.7 %all-to-all-start.1 = ((bf16[3072,16,2]{0,2,1:T(2,128)(2,1)}), bf16[3072,16,2]{0,2,1:T(2,128)(2,1)S(1)}, u32[]{:S(2)}, u32[]{:S(2)}) async-start(bf16[3072,16,2]{0,2,1:T(2,128)(2,1)} %convert_element_type.42), calls=%async_computation.2 | async-start | bytes 393216 | tf_op jit(solution)/shard_map/all_to_all | solution.py:60
  58.7 0.1 copy.24
  58.7 0.1 copy.23
  58.8 0.0 copy-done.1
  58.8 0.0 copy-done.2
  58.9 9.0 %all-to-all-done.1 = bf16[3072,16,2]{0,2,1:T(2,128)(2,1)S(1)} async-done(((bf16[3072,16,2]{0,2,1:T(2,128)(2,1)}), bf16[3072,16,2]{0,2,1:T(2,128)(2,1)S(1)}, u32[]{:S(2)}, u32[]{:S(2)}) %all-to-all-start.1) | async-done | bytes 196640 | tf_op jit(solution)/shard_map/all_to_all | solution.py:60
  67.8 1.3 %fusion.6 = bf16[64,3072]{1,0:T(8,128)(2,1)} fusion(bf16[3072,16,2]{0,2,1:T(2,128)(2,1)S(1)} %all-to-all-done.1, f32[64,16]{0,1:T(8,128)S(1)} %select_reduce_fusion, s32[64,16]{0,1:T(8,128)S(1)} %copy.23, pred[64,16]{0,1:T(8,128)(4,1)S(1)} %copy.24), kind=kOutput, calls=%fused_computation.10 | convolution fusion | flops 75700224 | bytes 599040 | tf_op jit(solution)/shard_map/dot_general | solution.py:68
  (9 shorter events, 0.1 us)
Async XLA Ops:
  6.5 5.6 %copy-start = (bf16[64,3072]{1,0:T(8,128)(2,1)S(1)}, bf16[64,3072]{1,0:T(8,128)(2,1)}, u32[]{:S(2)}) copy-start(bf16[64,3072]{1,0:T(8,128)(2,1)} %param.6) | copy-start | bytes 1179652
  6.5 43.7 %reduce-scatter.2.cloned.1.call-start = ((), (), s32[]{:S(2)}) async-start(), calls=%async_computation.3 | async-start | bytes 589824 | tf_op jit(solution)/shard_map/reduce_scatter | solution.py:52
  36.1 22.7 %copy-start.1 = (s32[64,8]{0,1:T(8,128)S(1)}, s32[64,8]{0,1:T(8,128)}, u32[]{:S(2)}) copy-start(s32[64,8]{0,1:T(8,128)} %param.7) | copy-start | bytes 6148
  36.1 22.7 %copy-start.2 = (f32[64,8]{0,1:T(8,128)S(1)}, f32[64,8]{0,1:T(8,128)}, u32[]{:S(2)}) copy-start(f32[64,8]{0,1:T(8,128)} %param.8) | copy-start | bytes 6148
  51.9 15.9 %all-to-all-start.1 = ((bf16[3072,16,2]{0,2,1:T(2,128)(2,1)}), bf16[3072,16,2]{0,2,1:T(2,128)(2,1)S(1)}, u32[]{:S(2)}, u32[]{:S(2)}) async-start(bf16[3072,16,2]{0,2,1:T(2,128)(2,1)} %convert_element_type.42), calls=%async_computation.2 | async-start | bytes 393216 | tf_op jit(solution)/shard_map/all_to_all | solution.py:60
Sparse Core Ops, SparseCore 0:
  44.6 5.5 reduce-scatter.1
where the time goes:
time: 76.2 us; the launch traced here: 75.9 us
  blocking collectives  18.9 us (25%)
  waiting for transfers between devices  14.7 us (19%)
  matrix products  13.6 us (18%)
  between operations  13.5 us (18%)
  local copies, waits for them, and re-layouts  7.31 us (10%)
  starting transfers between devices  6.74 us (9%)
  other arithmetic  1.2 us (2%)
    all_to_all x1, blocking collectives, body(): lax.all_to_all(outgoing.reshape(holders, SEND, outgoing.shape[1]), 'exper...  16.8 us
    all_to_all x1, waiting for transfers between devices, body(): lax.all_to_all(summed.reshape(feature_rows, holders, SEND).astype(jnp.bfl...  8.96 us
    dot_general x1, matrix products, body(): lax.dot_general(down_mat, hidden, (((1,), (1,)), ((), ())), preferred_ele...  8.41 us
    all_to_all x1, starting transfers between devices, body(): lax.all_to_all(summed.reshape(feature_rows, holders, SEND).astype(jnp.bfl...  6.74 us
    reduce_scatter x1, waiting for transfers between devices, body(): lax.psum_scatter(lax.dot_general(down_mat, hidden, (((1,), (1,)), ((), ()...  5.72 us
    scatter x1, local copies, waits for them, and re-layouts, body(): slot_table = jnp.full((capacity + 1,), tok_rows, jnp.int32).at[slot_of.re...  4.3 us
    dot_general x1, matrix products, body(): gate_val = jnp.dot(segment, gate_mat, preferred_element_type=jnp.float32)  3.94 us
    all_gather x1, blocking collectives, body(): segment = lax.all_gather(selected, 'width', axis=1, tiled=True)  2.09 us
  transfers between devices with their start and end apart: 2, of which 2 were waited for; matrix products, arithmetic and copies ran while one was open for 0% of the time, Pallas kernels for 0%

commit v1 on v0

v1 whole, which is shorter than its diff:
```python
import functools

import jax
import jax.numpy as jnp
from jax import lax
from jax.experimental import pallas as pl
from jax.experimental.pallas import tpu as pltpu
from jax.sharding import PartitionSpec as P

SEND = 2
VMEM = pl.BlockSpec(memory_space=pltpu.VMEM)
F32 = jnp.float32
BF16 = jnp.bfloat16


def params(mib):
    return pltpu.CompilerParams(vmem_limit_bytes=mib << 20)


def route_kernel(ids_ref, weight_ref, tokens_ref, outgoing_ref, coeff_ref):
    slots, rows = coeff_ref.shape
    slot = lax.broadcasted_iota(jnp.int32, (slots, rows), 0)
    expert, rank = slot // SEND, slot % SEND
    hits = jnp.zeros((slots, rows), F32)
    weight = jnp.zeros((slots, rows), F32)
    for k in range(ids_ref.shape[0]):
        hit = ids_ref[k : k + 1, :] == expert
        hits = jnp.where(hit, 1.0, hits)
        weight = jnp.where(hit, weight_ref[k : k + 1, :], weight)
    earlier = lax.broadcasted_iota(jnp.int32, (rows, rows), 0) < lax.broadcasted_iota(
        jnp.int32, (rows, rows), 1
    )
    ranking = jnp.dot(hits.astype(BF16), earlier.astype(BF16), preferred_element_type=F32)
    taken = jnp.logical_and(hits > 0.0, ranking == rank.astype(F32))
    coeff_ref[...] = jnp.where(taken, weight, 0.0)
    outgoing_ref[...] = jnp.dot(
        taken.astype(BF16), tokens_ref[...], preferred_element_type=F32
    ).astype(BF16)


def expert_kernel(width, *refs):
    rows = refs[:width]
    gate_ref, up_ref, down_ref = refs[width : width + 3]
    parts = refs[width + 3 :]
    features = rows[0].shape[1]
    me = lax.axis_index("width")
    gate = up = 0.0
    for d in range(width):
        block = pl.ds(pl.multiple_of(lax.rem(me + width - d, width) * features, features), features)
        x = rows[d][...]
        gate += jnp.dot(x, gate_ref[0, block, :], preferred_element_type=F32)
        up += jnp.dot(x, up_ref[0, block, :], preferred_element_type=F32)
    hidden = (gate / (1.0 + jnp.exp(-gate)) * up).astype(BF16)
    for d in range(width):
        block = pl.ds(pl.multiple_of(lax.rem(me + d, width) * features, features), features)
        parts[d][...] = lax.dot_general(
            hidden, down_ref[0, block, :], (((1,), (1,)), ((), ())), preferred_element_type=F32
        ).astype(BF16)


def combine_kernel(coeff_ref, returned_ref, mixed_ref):
    coeff = coeff_ref[...]
    high = coeff.astype(BF16)
    low = (coeff - high.astype(F32)).astype(BF16)
    returned = returned_ref[...]
    dims = (((0,), (0,)), ((), ()))
    mixed_ref[...] = (
        lax.dot_general(high, returned, dims, preferred_element_type=F32)
        + lax.dot_general(low, returned, dims, preferred_element_type=F32)
    ).astype(BF16)


def body(tokens, expert_ids, route_weight, gate_weight, up_weight, down_weight):
    holders, width = lax.axis_size("expert"), lax.axis_size("width")
    rows, features = tokens.shape
    slots = holders * SEND
    outgoing, coeff = pl.pallas_call(
        route_kernel,
        out_shape=(
            jax.ShapeDtypeStruct((slots, features), BF16),
            jax.ShapeDtypeStruct((slots, rows), F32),
        ),
        in_specs=[VMEM] * 3,
        out_specs=(VMEM, VMEM),
        compiler_params=params(8),
        name="route",
    )(expert_ids.T, route_weight.T, tokens)

    def exchange(x):
        return lax.all_to_all(
            x.reshape(holders, SEND, features), "expert", split_axis=0, concat_axis=0, tiled=True
        ).reshape(slots, features)

    def shifted(x, d):
        return lax.ppermute(x, "width", [(i, (i + d) % width) for i in range(width)])

    arrived = exchange(outgoing)
    blocks = [arrived] + [shifted(arrived, d) for d in range(1, width)]
    weights = [
        pltpu.with_memory_space_constraint(w, pltpu.VMEM)
        for w in (gate_weight, up_weight, down_weight)
    ]
    parts = pl.pallas_call(
        functools.partial(expert_kernel, width),
        out_shape=[jax.ShapeDtypeStruct((slots, features), BF16)] * width,
        in_specs=[VMEM] * (width + 3),
        out_specs=[VMEM] * width,
        compiler_params=params(24),
        name="experts",
    )(*blocks, *weights)
    summed = parts[0].astype(F32)
    for d in range(1, width):
        summed = summed + shifted(parts[d], d).astype(F32)
    returned = exchange(summed.astype(BF16))
    return pl.pallas_call(
        combine_kernel,
        out_shape=jax.ShapeDtypeStruct((rows, features), BF16),
        in_specs=[VMEM] * 2,
        out_specs=VMEM,
        compiler_params=params(8),
        name="combine",
    )(coeff, returned)


def solution(mesh):
    in_specs = (
        P("expert", "width"),
        P("expert", None),
        P("expert", None),
        P("expert", None, "width"),
        P("expert", None, "width"),
        P("expert", None, "width"),
    )
    out_specs = P("expert", "width")
    return jax.shard_map(body, mesh=mesh, in_specs=in_specs, out_specs=out_specs, check_vma=False)
```

time: 76.2 us -> 48.9 us (0.64)
  matrix products: 13.6 us -> 0 us
  between operations: 13.5 us -> 0.05 us
  waiting for transfers between devices: 14.7 us -> 2.73 us
  blocking collectives: 18.9 us -> 28.9 us
  starting transfers between devices: 6.74 us -> 0.24 us
  Pallas kernels: 0 us -> 5.54 us
  local copies, waits for them, and re-layouts: 7.31 us -> 11 us
  other arithmetic: 1.2 us -> 0.05 us
    dot_general x3 -> x0, matrix products: 13.6 us -> none  [the longest x1 8.41 us: body(): lax.dot_general(down_mat, hidden, (((1,), (1,)), ((), ())), preferred_ele...]
    all_to_all x1 -> x2, blocking collectives: 16.8 us -> 28.9 us  [exchange(): lax.all_to_all(x.reshape(holders, SEND, features), 'expert', split_axis=0...]
    unnamed x6 -> x12, local copies, waits for them, and re-layouts: 0.02 us -> 10.7 us
    all_to_all x1 -> x0, waiting for transfers between devices: 8.96 us -> none  [body(): lax.all_to_all(summed.reshape(feature_rows, holders, SEND).astype(jnp.bfl...]
    all_to_all x1 -> x0, starting transfers between devices: 6.74 us -> none  [body(): lax.all_to_all(summed.reshape(feature_rows, holders, SEND).astype(jnp.bfl...]
    reduce_scatter x1 -> x0, waiting for transfers between devices: 5.72 us -> none  [body(): lax.psum_scatter(lax.dot_general(down_mat, hidden, (((1,), (1,)), ((), ()...]
    pallas_call x0 -> x3, Pallas kernels: none -> 5.54 us  [the longest x1 4.09 us: body(): pl.pallas_call(functools.partial(expert_kernel, width), out_shape=[jax.Sh...]
    scatter x1 -> x0, local copies, waits for them, and re-layouts: 4.3 us -> none  [body(): slot_table = jnp.full((capacity + 1,), tok_rows, jnp.int32).at[slot_of.re...]
where the time goes in v1:
time: 48.9 us; the launch traced here: 48.5 us
  blocking collectives  28.9 us (59%)
  local copies, waits for them, and re-layouts  11 us (22%)
  Pallas kernels  5.54 us (11%)
  waiting for transfers between devices  2.73 us (6%)
    all_to_all x2, blocking collectives, exchange(): lax.all_to_all(x.reshape(holders, SEND, features), 'expert', split_axis=0...  28.9 us
    unnamed x12, local copies, waits for them, and re-layouts  10.7 us
    pallas_call x1, Pallas kernels, body(): pl.pallas_call(functools.partial(expert_kernel, width), out_shape=[jax.Sh...  4.09 us
    ppermute x2, waiting for transfers between devices, shifted(): lax.ppermute(x, 'width', [(i, (i + d) % width) for i in range(width)])  2.73 us
    pallas_call x1, Pallas kernels, body(): pl.pallas_call(combine_kernel, out_shape=jax.ShapeDtypeStruct((rows, feat...  1.13 us
  transfers between devices with their start and end apart: 2, of which 2 were waited for; matrix products, arithmetic and copies ran while one was open for 0% of the time, Pallas kernels for 0%

profile of v1, /device:TPU:0, one launch (start us, length us, event | category | flops | bytes accessed | tf_op | source)
XLA Modules:
  0.0 48.5 jit_solution(9690665884248737541)
XLA Ops:
  0.0 0.0 copy-start.3
  0.0 1.0 %copy-done.3 = bf16[64,3072]{1,0:T(8,128)(2,1)S(1)} copy-done((bf16[64,3072]{1,0:T(8,128)(2,1)S(1)}, bf16[64,3072]{1,0:T(8,128)(2,1)}, u32[]{:S(2)}) %copy-start.3) | copy-done | bytes 393240
  1.0 0.0 copy-start.4
  1.0 0.7 %copy-done.4 = s32[64,8]{0,1:T(8,128)S(1)} copy-done((s32[64,8]{0,1:T(8,128)S(1)}, s32[64,8]{0,1:T(8,128)}, u32[]{:S(2)}) %copy-start.4) | copy-done | bytes 2072
  1.7 0.0 copy-start.5
  1.7 0.7 %copy-done.5 = f32[64,8]{0,1:T(8,128)S(1)} copy-done((f32[64,8]{0,1:T(8,128)S(1)}, f32[64,8]{0,1:T(8,128)}, u32[]{:S(2)}) %copy-start.5) | copy-done | bytes 2072
  2.4 0.3 route.1
  2.7 0.1 reshape.12
  2.8 16.8 %all_to_all.10 = bf16[16,2,3072]{2,1,0:T(2,128)(2,1)S(1)} all-to-all(bf16[16,2,3072]{2,1,0:T(2,128)(2,1)S(1)} %reshape.12), channel_id=1, replica_groups=mesh['expert'=16,'width'=2] {'expert'}, dimensions={0} | all-to-all | bytes 393216 | tf_op jit(solution)/shard_map/all_to_all | solution.py:90
  19.6 0.1 reshape.13.refs_0_
  19.6 0.1 collective-permute-start
  19.7 1.4 %collective-permute-done.refs_1_ = bf16[32,3072]{1,0:T(8,128)(2,1)S(1)} collective-permute-done((bf16[32,3072]{1,0:T(8,128)(2,1)S(1)}, bf16[32,3072]{1,0:T(8,128)(2,1)S(1)}, u32[]{:S(2)}, u32[]{:S(2)}) %collective-permute-start) | collective-permute-done | bytes 196640 | tf_op jit(solution)/shard_map/ppermute | solution.py:95
  21.1 0.0 copy-start
  21.1 2.8 %copy-done = bf16[1,6144,512]{2,1,0:T(8,128)(2,1)S(1)} copy-done((bf16[1,6144,512]{2,1,0:T(8,128)(2,1)S(1)}, bf16[1,6144,512]{2,1,0:T(8,128)(2,1)}, u32[]{:S(2)}) %copy-start) | copy-done | bytes 6291480
  23.9 0.0 copy-start.1
  23.9 2.8 %copy-done.1 = bf16[1,6144,512]{2,1,0:T(8,128)(2,1)S(1)} copy-done((bf16[1,6144,512]{2,1,0:T(8,128)(2,1)S(1)}, bf16[1,6144,512]{2,1,0:T(8,128)(2,1)}, u32[]{:S(2)}) %copy-start.1) | copy-done | bytes 6291480
  26.7 0.0 copy-start.2
  26.7 2.8 %copy-done.2 = bf16[1,6144,512]{2,1,0:T(8,128)(2,1)S(1)} copy-done((bf16[1,6144,512]{2,1,0:T(8,128)(2,1)S(1)}, bf16[1,6144,512]{2,1,0:T(8,128)(2,1)}, u32[]{:S(2)}) %copy-start.2) | copy-done | bytes 6291480
  29.5 4.1 %experts.1 = (bf16[32,3072]{1,0:T(8,128)(2,1)S(1)}, bf16[32,3072]{1,0:T(8,128)(2,1)S(1)}) custom-call(bf16[32,3072]{1,0:T(8,128)(2,1)S(1)} %reshape.13.refs_0_, bf16[32,3072]{1,0:T(8,128)(2,1)S(1)} %collective-permute-done.refs_1_, bf16[1,6144,512]{2,1,0:T(8,128)(2,1)S(1)} %copy-done, bf16[1,6144,512]{2,1,0:T(8,128)(2,1)S(1)} %copy-done.1, ...), custom_call_target="tpu_custom_call" | custom-call | tf_op jit(solution)/shard_map/experts/pallas_call | solution.py:103
  33.6 0.2 collective-permute-start.1
  33.8 1.3 %collective-permute-done.1 = bf16[32,3072]{1,0:T(8,128)(2,1)S(1)} collective-permute-done((bf16[32,3072]{1,0:T(8,128)(2,1)S(1)}, bf16[32,3072]{1,0:T(8,128)(2,1)S(1)}, u32[]{:S(2)}, u32[]{:S(2)}) %collective-permute-start.1) | collective-permute-done | bytes 196640 | tf_op jit(solution)/shard_map/ppermute | solution.py:95
  35.1 0.1 reshape.14
  35.2 12.1 %all_to_all.11 = bf16[16,2,3072]{2,1,0:T(2,128)(2,1)S(1)} all-to-all(bf16[16,2,3072]{2,1,0:T(2,128)(2,1)S(1)} %reshape.14), channel_id=1, replica_groups=mesh['expert'=16,'width'=2] {'expert'}, dimensions={0} | all-to-all | bytes 393216 | tf_op jit(solution)/shard_map/all_to_all | solution.py:90
  47.3 0.1 reshape.15.returned_ref
  47.4 1.1 %combine.1 = bf16[64,3072]{1,0:T(8,128)(2,1)} custom-call(f32[32,64]{1,0:T(8,128)S(1)} %get-tuple-element.9.coeff_ref, bf16[32,3072]{1,0:T(8,128)(2,1)S(1)} %reshape.15.returned_ref), custom_call_target="tpu_custom_call" | custom-call | tf_op jit(solution)/shard_map/combine/pallas_call | solution.py:115
  (1 shorter events, 0.0 us)
Async XLA Ops:
  0.0 1.0 %copy-start.3 = (bf16[64,3072]{1,0:T(8,128)(2,1)S(1)}, bf16[64,3072]{1,0:T(8,128)(2,1)}, u32[]{:S(2)}) copy-start(bf16[64,3072]{1,0:T(8,128)(2,1)} %tokens_ref.1) | copy-start | bytes 1179652
  1.0 0.7 %copy-start.4 = (s32[64,8]{0,1:T(8,128)S(1)}, s32[64,8]{0,1:T(8,128)}, u32[]{:S(2)}) copy-start(s32[64,8]{0,1:T(8,128)} %param.7) | copy-start | bytes 6148
  1.7 0.7 %copy-start.5 = (f32[64,8]{0,1:T(8,128)S(1)}, f32[64,8]{0,1:T(8,128)}, u32[]{:S(2)}) copy-start(f32[64,8]{0,1:T(8,128)} %param.8) | copy-start | bytes 6148
  19.6 1.5 %collective-permute-start = (bf16[32,3072]{1,0:T(8,128)(2,1)S(1)}, bf16[32,3072]{1,0:T(8,128)(2,1)S(1)}, u32[]{:S(2)}, u32[]{:S(2)}) collective-permute-start(bf16[32,3072]{1,0:T(8,128)(2,1)S(1)} %reshape.13.refs_0_), channel_id=1, source_target_pairs={{0,1},{1,0},{2,3},{3,2},{4,5},{5,4},{6,7},{7,6},{8,9},{9,8},{10,11... | collective-permute-start | bytes 589832 | tf_op jit(solution)/shard_map/ppermute | solution.py:95
  21.1 2.8 %copy-start = (bf16[1,6144,512]{2,1,0:T(8,128)(2,1)S(1)}, bf16[1,6144,512]{2,1,0:T(8,128)(2,1)}, u32[]{:S(2)}) copy-start(bf16[1,6144,512]{2,1,0:T(8,128)(2,1)} %refs_2_.1) | copy-start | bytes 18874372
  23.9 2.8 %copy-start.1 = (bf16[1,6144,512]{2,1,0:T(8,128)(2,1)S(1)}, bf16[1,6144,512]{2,1,0:T(8,128)(2,1)}, u32[]{:S(2)}) copy-start(bf16[1,6144,512]{2,1,0:T(8,128)(2,1)} %refs_3_.1) | copy-start | bytes 18874372
  26.7 2.8 %copy-start.2 = (bf16[1,6144,512]{2,1,0:T(8,128)(2,1)S(1)}, bf16[1,6144,512]{2,1,0:T(8,128)(2,1)}, u32[]{:S(2)}) copy-start(bf16[1,6144,512]{2,1,0:T(8,128)(2,1)} %refs_4_.1) | copy-start | bytes 18874372
  33.6 1.5 %collective-permute-start.1 = (bf16[32,3072]{1,0:T(8,128)(2,1)S(1)}, bf16[32,3072]{1,0:T(8,128)(2,1)S(1)}, u32[]{:S(2)}, u32[]{:S(2)}) collective-permute-start(bf16[32,3072]{1,0:T(8,128)(2,1)S(1)} %get-tuple-element.12), channel_id=1, source_target_pairs={{0,1},{1,0},{2,3},{3,2},{4,5},{5,4},{6,7},{7,6},{8,9},{9,8},{10,11... | collective-permute-start | bytes 589832 | tf_op jit(solution)/shard_map/ppermute | solution.py:95

commit v2 on v1

v2 whole, which is shorter than its diff:
```python
import functools

import jax
import jax.numpy as jnp
from jax import lax
from jax.experimental import pallas as pl
from jax.experimental.pallas import tpu as pltpu
from jax.sharding import PartitionSpec as P

SEND = 2
VMEM = pl.BlockSpec(memory_space=pltpu.VMEM)
HBM = pl.BlockSpec(memory_space=pltpu.HBM)
F32 = jnp.float32
BF16 = jnp.bfloat16


def params(mib):
    return pltpu.CompilerParams(vmem_limit_bytes=mib << 20)


def hint(micros):
    return pl.CostEstimate(flops=micros * 10**9, bytes_accessed=0, transcendentals=0)


def split_rows(ref, value):
    for e in range(ref.shape[0]):
        ref[e] = value[e * SEND : (e + 1) * SEND, :]


def join_rows(ref):
    return jnp.concatenate([ref[e] for e in range(ref.shape[0])], axis=0)


def slots_kernel(ids_hbm, weight_hbm, tokens_hbm, taken_ref, coeff_ref, tokens_ref, ids_ref, weight_ref, sems):
    copies = [
        pltpu.make_async_copy(source, target, sems.at[i])
        for i, (source, target) in enumerate(
            ((ids_hbm, ids_ref), (weight_hbm, weight_ref), (tokens_hbm, tokens_ref))
        )
    ]
    for copy in copies:
        copy.start()
    slots, rows = coeff_ref.shape
    slot = lax.broadcasted_iota(jnp.int32, (slots, rows), 0)
    expert, rank = slot // SEND, slot % SEND
    earlier = lax.broadcasted_iota(jnp.int32, (rows, rows), 0) < lax.broadcasted_iota(
        jnp.int32, (rows, rows), 1
    )
    hits = jnp.zeros((slots, rows), F32)
    weight = jnp.zeros((slots, rows), F32)
    copies[0].wait()
    copies[1].wait()
    for k in range(ids_ref.shape[0]):
        hit = ids_ref[k : k + 1, :] == expert
        hits = jnp.where(hit, 1.0, hits)
        weight = jnp.where(hit, weight_ref[k : k + 1, :], weight)
    ranking = jnp.dot(hits.astype(BF16), earlier.astype(BF16), preferred_element_type=F32)
    taken = jnp.logical_and(hits > 0.0, ranking == rank.astype(F32))
    coeff_ref[...] = jnp.where(taken, weight, 0.0)
    taken_ref[...] = jnp.where(taken, 1.0, 0.0).astype(BF16)
    copies[2].wait()


def select_kernel(taken_ref, tokens_ref, outgoing_ref):
    split_rows(
        outgoing_ref,
        jnp.dot(taken_ref[...], tokens_ref[...], preferred_element_type=F32).astype(BF16),
    )


def feature_block(d, features):
    width = lax.axis_size("width")
    owner = lax.rem(lax.axis_index("width") + width - d, width)
    return pl.ds(pl.multiple_of(owner * features, features), features)


def own_kernel(rows_ref, gate_ref, up_ref, gate_out, up_out):
    x = join_rows(rows_ref)
    block = feature_block(0, x.shape[1])
    gate_out[...] = jnp.dot(x, gate_ref[0, block, :], preferred_element_type=F32)
    up_out[...] = jnp.dot(x, up_ref[0, block, :], preferred_element_type=F32)


def down_block(hidden, down_ref, d, features):
    return lax.dot_general(
        hidden,
        down_ref[0, feature_block(d, features), :],
        (((1,), (1,)), ((), ())),
        preferred_element_type=F32,
    ).astype(BF16)


def others_kernel(others, *refs):
    rows = refs[:others]
    gate_in, up_in, gate_ref, up_ref, down_ref = refs[others : others + 5]
    hidden_ref = refs[others + 5]
    parts = refs[others + 6 :]
    gate, up = gate_in[...], up_in[...]
    for d in range(others):
        x = join_rows(rows[d])
        block = feature_block(d + 1, x.shape[1])
        gate += jnp.dot(x, gate_ref[0, block, :], preferred_element_type=F32)
        up += jnp.dot(x, up_ref[0, block, :], preferred_element_type=F32)
    hidden = (gate / (1.0 + jnp.exp(-gate)) * up).astype(BF16)
    hidden_ref[...] = hidden
    for d in range(others):
        parts[d][...] = down_block(hidden, down_ref, d + 1, parts[d].shape[1])


def own_part_kernel(hidden_ref, down_ref, part_ref):
    part_ref[...] = down_block(hidden_ref[...], down_ref, 0, part_ref.shape[1])


def combine_kernel(coeff_ref, returned_ref, mixed_ref):
    coeff = coeff_ref[...]
    high = coeff.astype(BF16)
    low = (coeff - high.astype(F32)).astype(BF16)
    returned = join_rows(returned_ref)
    dims = (((0,), (0,)), ((), ()))
    mixed_ref[...] = (
        lax.dot_general(high, returned, dims, preferred_element_type=F32)
        + lax.dot_general(low, returned, dims, preferred_element_type=F32)
    ).astype(BF16)


def body(tokens, expert_ids, route_weight, gate_weight, up_weight, down_weight):
    holders, width = lax.axis_size("expert"), lax.axis_size("width")
    rows, features = tokens.shape
    top = expert_ids.shape[1]
    hidden_units = gate_weight.shape[2]
    slots = holders * SEND
    shape = jax.ShapeDtypeStruct

    ids, weights, tokens = (
        pltpu.with_memory_space_constraint(x, pltpu.HBM)
        for x in (expert_ids.T, route_weight.T, tokens)
    )
    taken, coeff, tokens = pl.pallas_call(
        slots_kernel,
        out_shape=(
            shape((slots, rows), BF16),
            shape((slots, rows), F32),
            shape((rows, features), BF16),
        ),
        in_specs=[HBM] * 3,
        out_specs=[VMEM] * 3,
        scratch_shapes=[
            pltpu.VMEM((top, rows), jnp.int32),
            pltpu.VMEM((top, rows), F32),
            pltpu.SemaphoreType.DMA((3,)),
        ],
        compiler_params=params(8),
        name="slots",
    )(ids, weights, tokens)
    outgoing = pl.pallas_call(
        select_kernel,
        out_shape=shape((holders, SEND, features), BF16),
        in_specs=[VMEM] * 2,
        out_specs=VMEM,
        compiler_params=params(8),
        cost_estimate=hint(40),
        name="select",
    )(taken, tokens)

    def exchange(x):
        return lax.all_to_all(x, "expert", split_axis=0, concat_axis=0, tiled=True)

    def shifted(x, d):
        return lax.ppermute(x, "width", [(i, (i + d) % width) for i in range(width)])

    arrived = exchange(outgoing)
    others = [shifted(arrived, d) for d in range(1, width)]
    gate_vmem, up_vmem, down_vmem = (
        pltpu.with_memory_space_constraint(w, pltpu.VMEM)
        for w in (gate_weight, up_weight, down_weight)
    )
    gate, up = pl.pallas_call(
        own_kernel,
        out_shape=[shape((slots, hidden_units), F32)] * 2,
        in_specs=[VMEM] * 3,
        out_specs=[VMEM] * 2,
        compiler_params=params(20),
        cost_estimate=hint(2),
        name="own",
    )(arrived, gate_vmem, up_vmem)
    hidden, *parts = pl.pallas_call(
        functools.partial(others_kernel, width - 1),
        out_shape=[shape((slots, hidden_units), BF16)]
        + [shape((slots, features), BF16)] * (width - 1),
        in_specs=[VMEM] * (width + 4),
        out_specs=[VMEM] * width,
        compiler_params=params(24),
        cost_estimate=hint(2),
        name="others",
    )(*others, gate, up, gate_vmem, up_vmem, down_vmem)
    received = [shifted(part, d + 1) for d, part in enumerate(reversed(parts))]
    summed = pl.pallas_call(
        own_part_kernel,
        out_shape=shape((slots, features), BF16),
        in_specs=[VMEM] * 2,
        out_specs=VMEM,
        compiler_params=params(20),
        cost_estimate=hint(2),
        name="own_part",
    )(hidden, down_vmem).astype(F32)
    for part in received:
        summed = summed + part.astype(F32)
    returned = exchange(summed.astype(BF16).reshape(holders, SEND, features))
    return pl.pallas_call(
        combine_kernel,
        out_shape=shape((rows, features), BF16),
        in_specs=[VMEM] * 2,
        out_specs=VMEM,
        compiler_params=params(8),
        name="combine",
    )(coeff, returned)


def solution(mesh):
    in_specs = (
        P("expert", "width"),
        P("expert", None),
        P("expert", None),
        P("expert", None, "width"),
        P("expert", None, "width"),
        P("expert", None, "width"),
    )
    out_specs = P("expert", "width")
    return jax.shard_map(body, mesh=mesh, in_specs=in_specs, out_specs=out_specs, check_vma=False)
```

time: 48.9 us -> 37.2 us (0.76)
  local copies, waits for them, and re-layouts: 11 us -> 0.24 us
  waiting for transfers between devices: 2.73 us -> 0.53 us
  Pallas kernels: 5.54 us -> 6.72 us
    unnamed x12 -> x8, local copies, waits for them, and re-layouts: 10.7 us -> 0.17 us
    ppermute x2, waiting for transfers between devices: 2.73 us -> 0.53 us  [shifted(): lax.ppermute(x, 'width', [(i, (i + d) % width) for i in range(width)])]
    pallas_call x3 -> x6, Pallas kernels: 5.54 us -> 6.72 us  [the longest x1 2.13 us: body(): pl.pallas_call(functools.partial(others_kernel, width - 1), out_shape=[sh...]
  transfers between devices with their start and end apart: 2 -> 2, of which waited for: 2 -> 2; matrix products, arithmetic and copies ran while one was open for 0% -> 0% of each run, Pallas kernels for 0% -> 6%
where the time goes in v2:
time: 37.2 us; the launch traced here: 36.9 us
  blocking collectives  29.2 us (78%)
  Pallas kernels  6.72 us (18%)
  waiting for transfers between devices  0.53 us (1%)
    all_to_all x2, blocking collectives, exchange(): return lax.all_to_all(x, 'expert', split_axis=0, concat_axis=0, tiled=True)  29.2 us
    pallas_call x1, Pallas kernels, body(): pl.pallas_call(functools.partial(others_kernel, width - 1), out_shape=[sh...  2.13 us
    pallas_call x1, Pallas kernels, body(): pl.pallas_call(own_kernel, out_shape=[shape((slots, hidden_units), F32)]...  1.18 us
    pallas_call x1, Pallas kernels, body(): pl.pallas_call(combine_kernel, out_shape=shape((rows, features), BF16), i...  1.15 us
    pallas_call x1, Pallas kernels, body(): pl.pallas_call(slots_kernel, out_shape=(shape((slots, rows), BF16), shape...  1.05 us
    pallas_call x1, Pallas kernels, body(): pl.pallas_call(own_part_kernel, out_shape=shape((slots, features), BF16),...  1.01 us
  transfers between devices with their start and end apart: 2, of which 2 were waited for; matrix products, arithmetic and copies ran while one was open for 0% of the time, Pallas kernels for 6%

profile of v2, /device:TPU:0, one launch (start us, length us, event | category | flops | bytes accessed | tf_op | source)
XLA Modules:
  0.0 36.9 jit_solution(212888935523059550)
XLA Ops:
  0.0 1.1 %slots.1 = (bf16[32,64]{1,0:T(8,128)(2,1)S(1)}, f32[32,64]{1,0:T(8,128)S(1)}, bf16[64,3072]{1,0:T(8,128)(2,1)S(1)}) custom-call(s32[8,64]{1,0:T(8,128)} %bitcast.4, f32[8,64]{1,0:T(8,128)} %bitcast.5, bf16[64,3072]{1,0:T(8,128)(2,1)} %tokens_hbm.1), custom_call_target="tpu_custom_call" | custom-call | tf_op jit(solution)/shard_map/slots/pallas_call | solution.py:138
  1.1 0.0 copy-start
  1.1 0.0 copy-start.1
  1.1 0.2 select.1
  1.3 0.0 slice-start
  1.3 17.0 %all_to_all.10.rows_ref = bf16[16,2,3072]{2,1,0:T(2,128)(2,1)S(1)} all-to-all(bf16[16,2,3072]{2,1,0:T(2,128)(2,1)S(1)} %select.1), channel_id=1, replica_groups=mesh['expert'=16,'width'=2] {'expert'}, dimensions={0} | all-to-all | bytes 393216 | tf_op jit(solution)/shard_map/all_to_all | solution.py:166
  18.3 0.0 slice-start.1
  18.4 0.0 collective-permute-start
  18.4 0.0 copy-done
  18.4 0.0 copy-done.1
  18.4 1.2 %own.1 = (f32[32,512]{1,0:T(8,128)S(1)}, f32[32,512]{1,0:T(8,128)S(1)}) custom-call(bf16[16,2,3072]{2,1,0:T(2,128)(2,1)S(1)} %all_to_all.10.rows_ref, bf16[1,6144,512]{2,1,0:T(8,128)(2,1)S(1)} %copy-done, bf16[1,6144,512]{2,1,0:T(8,128)(2,1)S(1)} %copy-done.1), custom_call_target="tpu_custom_call" | custom-call | flops 2000000000 | tf_op jit(solution)/shard_map/own/pallas_call | solution.py:177
  19.5 0.2 collective-permute-done.refs_0_
  19.8 0.0 slice-done
  19.8 0.1 slice-done.1
  19.9 2.1 %others.1 = (bf16[32,512]{1,0:T(8,128)(2,1)S(1)}, bf16[32,3072]{1,0:T(8,128)(2,1)S(1)}) custom-call(bf16[16,2,3072]{2,1,0:T(2,128)(2,1)S(1)} %collective-permute-done.refs_0_, f32[32,512]{1,0:T(8,128)S(1)} %get-tuple-element.15.refs_1_, f32[32,512]{1,0:T(8,128)S(1)} %get-tuple-element.16.refs_2_, bf16[1,6144,512]{2,1,0:T(8,128)(2,1)S(1)} %copy-done, ...), custom_call_target="tpu_custom_call" | custom-call | flops 2000000000 | tf_op jit(solution)/shard_map/others/pallas_call | solution.py:186
  22.1 0.2 collective-permute-start.1
  22.2 1.0 %own_part.1 = bf16[32,3072]{1,0:T(8,128)(2,1)S(1)} custom-call(bf16[32,512]{1,0:T(8,128)(2,1)S(1)} %get-tuple-element.17.hidden_ref, bf16[1,6144,512]{2,1,0:T(8,128)(2,1)S(1)} %bitcast.3), custom_call_target="tpu_custom_call" | custom-call | flops 2000000000 | tf_op jit(solution)/shard_map/own_part/pallas_call | solution.py:197
  23.3 0.3 collective-permute-done.1
  23.6 0.1 reshape.3
  23.7 12.1 %all_to_all.11.returned_ref = bf16[16,2,3072]{2,1,0:T(2,128)(2,1)S(1)} all-to-all(bf16[16,2,3072]{2,1,0:T(2,128)(2,1)S(1)} %reshape.3), channel_id=1, replica_groups=mesh['expert'=16,'width'=2] {'expert'}, dimensions={0} | all-to-all | bytes 393216 | tf_op jit(solution)/shard_map/all_to_all | solution.py:166
  35.8 1.1 %combine.1 = bf16[64,3072]{1,0:T(8,128)(2,1)} custom-call(f32[32,64]{1,0:T(8,128)S(1)} %get-tuple-element.12.coeff_ref, bf16[16,2,3072]{2,1,0:T(2,128)(2,1)S(1)} %all_to_all.11.returned_ref), custom_call_target="tpu_custom_call" | custom-call | tf_op jit(solution)/shard_map/combine/pallas_call | solution.py:209
  (2 shorter events, 0.0 us)
Async XLA Ops:
  1.1 17.3 %copy-start = (bf16[1,6144,512]{2,1,0:T(8,128)(2,1)S(1)}, bf16[1,6144,512]{2,1,0:T(8,128)(2,1)}, u32[]{:S(2)}) copy-start(bf16[1,6144,512]{2,1,0:T(8,128)(2,1)} %refs_3_.1) | copy-start | bytes 18874372
  1.1 17.3 %copy-start.1 = (bf16[1,6144,512]{2,1,0:T(8,128)(2,1)S(1)}, bf16[1,6144,512]{2,1,0:T(8,128)(2,1)}, u32[]{:S(2)}) copy-start(bf16[1,6144,512]{2,1,0:T(8,128)(2,1)} %refs_4_.1) | copy-start | bytes 18874372
  1.3 18.5 %slice-start = ((s8[6291456]{0:T(1024)(128)(4,1)}), s8[4194304]{0:T(1024)(128)(4,1)S(1)}, s32[]{:S(2)}) async-start(s8[6291456]{0:T(1024)(128)(4,1)} %bitcast.2), calls=%async_computation.2 | async-start | bytes 8388608
  18.3 1.6 %slice-start.1 = ((s8[6291456]{0:T(1024)(128)(4,1)}), s8[2097152]{0:T(1024)(128)(4,1)S(1)}, s32[]{:S(2)}) async-start(s8[6291456]{0:T(1024)(128)(4,1)} %bitcast.2), calls=%async_computation.3 | async-start | bytes 4194304
  18.4 1.4 %collective-permute-start = (bf16[16,2,3072]{2,1,0:T(2,128)(2,1)S(1)}, bf16[16,2,3072]{2,1,0:T(2,128)(2,1)S(1)}, u32[]{:S(2)}, u32[]{:S(2)}) collective-permute-start(bf16[16,2,3072]{2,1,0:T(2,128)(2,1)S(1)} %all_to_all.10.rows_ref), channel_id=1, source_target_pairs={{0,1},{1,0},{2,3},{3,2},{4,5},{5,4},{6,7},{7,6},{8,9},{9,8},{10,11... | collective-permute-start | bytes 589832 | tf_op jit(solution)/shard_map/ppermute | solution.py:169
  22.1 1.5 %collective-permute-start.1 = (bf16[32,3072]{1,0:T(8,128)(2,1)S(1)}, bf16[32,3072]{1,0:T(8,128)(2,1)S(1)}, u32[]{:S(2)}, u32[]{:S(2)}) collective-permute-start(bf16[32,3072]{1,0:T(8,128)(2,1)S(1)} %get-tuple-element.18), channel_id=1, source_target_pairs={{0,1},{1,0},{2,3},{3,2},{4,5},{5,4},{6,7},{7,6},{8,9},{9,8},{10,11... | collective-permute-start | bytes 589832 | tf_op jit(solution)/shard_map/ppermute | solution.py:169

commit v3 on v2

--- a/solution.py
+++ b/solution.py
@@ -8,6 +8,7 @@
 from jax.sharding import PartitionSpec as P
 
 SEND = 2
+LANES = 128
 VMEM = pl.BlockSpec(memory_space=pltpu.VMEM)
 HBM = pl.BlockSpec(memory_space=pltpu.HBM)
 F32 = jnp.float32
@@ -23,12 +24,15 @@
 
 
 def split_rows(ref, value):
-    for e in range(ref.shape[0]):
-        ref[e] = value[e * SEND : (e + 1) * SEND, :]
-
-
-def join_rows(ref):
-    return jnp.concatenate([ref[e] for e in range(ref.shape[0])], axis=0)
+    piece = ref.shape[2]
+    pieces = value.shape[1] // piece
+    for i in range(ref.shape[0]):
+        e, u = divmod(i, pieces)
+        ref[i] = value[e * SEND : (e + 1) * SEND, u * piece : (u + 1) * piece]
+
+
+def join_rows(ref, u, pieces):
+    return jnp.concatenate([ref[i] for i in range(u, ref.shape[0], pieces)], axis=0)
 
 
 def slots_kernel(ids_hbm, weight_hbm, tokens_hbm, taken_ref, coeff_ref, tokens_ref, ids_ref, weight_ref, sems):
@@ -68,59 +72,82 @@
     )
 
 
-def feature_block(d, features):
+def owned(d, features, pieces):
     width = lax.axis_size("width")
     owner = lax.rem(lax.axis_index("width") + width - d, width)
-    return pl.ds(pl.multiple_of(owner * features, features), features)
-
-
-def own_kernel(rows_ref, gate_ref, up_ref, gate_out, up_out):
-    x = join_rows(rows_ref)
-    block = feature_block(0, x.shape[1])
-    gate_out[...] = jnp.dot(x, gate_ref[0, block, :], preferred_element_type=F32)
-    up_out[...] = jnp.dot(x, up_ref[0, block, :], preferred_element_type=F32)
-
-
-def down_block(hidden, down_ref, d, features):
-    return lax.dot_general(
-        hidden,
-        down_ref[0, feature_block(d, features), :],
-        (((1,), (1,)), ((), ())),
-        preferred_element_type=F32,
-    ).astype(BF16)
-
-
-def others_kernel(others, *refs):
+    if pieces == 1:
+        return [pl.ds(pl.multiple_of(owner * features, features), features)]
+    piece = features // pieces
+    return [
+        pl.ds(pl.multiple_of(u * features + owner * piece, piece), piece) for u in range(pieces)
+    ]
+
+
+def gate_up(rows_ref, gate_ref, up_ref, d, pieces, gate, up):
+    for u, block in enumerate(owned(d, rows_ref.shape[2] * pieces, pieces)):
+        x = join_rows(rows_ref, u, pieces)
+        gate += jnp.dot(x, gate_ref[0, block, :], preferred_element_type=F32)
+        up += jnp.dot(x, up_ref[0, block, :], preferred_element_type=F32)
+    return gate, up
+
+
+def own_kernel(pieces, rows_ref, gate_ref, up_ref, down_ref, gate_out, up_out):
+    del down_ref
+    gate_out[...], up_out[...] = gate_up(rows_ref, gate_ref, up_ref, 0, pieces, 0.0, 0.0)
+
+
+def down_part(hidden, down_ref, d, pieces, part_ref):
+    features = part_ref.shape[1]
+    piece = features // pieces
+    for u, block in enumerate(owned(d, features, pieces)):
+        part_ref[:, u * piece : (u + 1) * piece] = lax.dot_general(
+            hidden, down_ref[0, block, :], (((1,), (1,)), ((), ())), preferred_element_type=F32
+        ).astype(BF16)
+
+
+def others_kernel(others, pieces, *refs):
     rows = refs[:others]
     gate_in, up_in, gate_ref, up_ref, down_ref = refs[others : others + 5]
     hidden_ref = refs[others + 5]
     parts = refs[others + 6 :]
     gate, up = gate_in[...], up_in[...]
     for d in range(others):
-        x = join_rows(rows[d])
-        block = feature_block(d + 1, x.shape[1])
-        gate += jnp.dot(x, gate_ref[0, block, :], preferred_element_type=F32)
-        up += jnp.dot(x, up_ref[0, block, :], preferred_element_type=F32)
+        gate, up = gate_up(rows[d], gate_ref, up_ref, d + 1, pieces, gate, up)
     hidden = (gate / (1.0 + jnp.exp(-gate)) * up).astype(BF16)
     hidden_ref[...] = hidden
     for d in range(others):
-        parts[d][...] = down_block(hidden, down_ref, d + 1, parts[d].shape[1])
-
-
-def own_part_kernel(hidden_ref, down_ref, part_ref):
-    part_ref[...] = down_block(hidden_ref[...], down_ref, 0, part_ref.shape[1])
-
-
-def combine_kernel(coeff_ref, returned_ref, mixed_ref):
+        down_part(hidden, down_ref, d + 1, pieces, parts[d])
+
+
+def own_part_kernel(pieces, hidden_ref, down_ref, part_ref):
+    down_part(hidden_ref[...], down_ref, 0, pieces, part_ref)
+
+
+def sum_kernel(*refs):
+    summed = refs[0][...].astype(F32)
+    for part in refs[1:-1]:
+        summed += part[...].astype(F32)
+    split_rows(refs[-1], summed.astype(BF16))
+
+
+def combine_kernel(pieces, coeff_ref, returned_ref, mixed_hbm, mixed_ref, sems):
     coeff = coeff_ref[...]
     high = coeff.astype(BF16)
     low = (coeff - high.astype(F32)).astype(BF16)
-    returned = join_rows(returned_ref)
     dims = (((0,), (0,)), ((), ()))
-    mixed_ref[...] = (
-        lax.dot_general(high, returned, dims, preferred_element_type=F32)
-        + lax.dot_general(low, returned, dims, preferred_element_type=F32)
-    ).astype(BF16)
+    piece = returned_ref.shape[2]
+    copies = []
+    for u in range(pieces):
+        returned = join_rows(returned_ref, u, pieces)
+        block = (slice(None), pl.ds(u * piece, piece))
+        mixed_ref[block] = (
+            lax.dot_general(high, returned, dims, preferred_element_type=F32)
+            + lax.dot_general(low, returned, dims, preferred_element_type=F32)
+        ).astype(BF16)
+        copies.append(pltpu.make_async_copy(mixed_ref.at[block], mixed_hbm.at[block], sems.at[u]))
+        copies[-1].start()
+    for copy in copies:
+        copy.wait()
 
 
 def body(tokens, expert_ids, route_weight, gate_weight, up_weight, down_weight):
@@ -129,6 +156,8 @@
     top = expert_ids.shape[1]
     hidden_units = gate_weight.shape[2]
     slots = holders * SEND
+    pieces = width if features % (width * LANES) == 0 else 1
+    sent = (holders * pieces, SEND, features // pieces)
     shape = jax.ShapeDtypeStruct
 
     ids, weights, tokens = (
@@ -154,7 +183,7 @@
     )(ids, weights, tokens)
     outgoing = pl.pallas_call(
         select_kernel,
-        out_shape=shape((holders, SEND, features), BF16),
+        out_shape=shape(sent, BF16),
         in_specs=[VMEM] * 2,
         out_specs=VMEM,
         compiler_params=params(8),
@@ -163,7 +192,8 @@
     )(taken, tokens)
 
     def exchange(x):
-        return lax.all_to_all(x, "expert", split_axis=0, concat_axis=0, tiled=True)
+        axes = "expert" if pieces == 1 else ("expert", "width")
+        return lax.all_to_all(x, axes, split_axis=0, concat_axis=0, tiled=True)
 
     def shifted(x, d):
         return lax.ppermute(x, "width", [(i, (i + d) % width) for i in range(width)])
@@ -175,16 +205,16 @@
         for w in (gate_weight, up_weight, down_weight)
     )
     gate, up = pl.pallas_call(
-        own_kernel,
+        functools.partial(own_kernel, pieces),
         out_shape=[shape((slots, hidden_units), F32)] * 2,
-        in_specs=[VMEM] * 3,
+        in_specs=[VMEM] * 4,
         out_specs=[VMEM] * 2,
         compiler_params=params(20),
         cost_estimate=hint(2),
         name="own",
-    )(arrived, gate_vmem, up_vmem)
+    )(arrived, gate_vmem, up_vmem, down_vmem)
     hidden, *parts = pl.pallas_call(
-        functools.partial(others_kernel, width - 1),
+        functools.partial(others_kernel, width - 1, pieces),
         out_shape=[shape((slots, hidden_units), BF16)]
         + [shape((slots, features), BF16)] * (width - 1),
         in_specs=[VMEM] * (width + 4),
@@ -194,23 +224,30 @@
         name="others",
     )(*others, gate, up, gate_vmem, up_vmem, down_vmem)
     received = [shifted(part, d + 1) for d, part in enumerate(reversed(parts))]
-    summed = pl.pallas_call(
-        own_part_kernel,
+    part = pl.pallas_call(
+        functools.partial(own_part_kernel, pieces),
         out_shape=shape((slots, features), BF16),
         in_specs=[VMEM] * 2,
         out_specs=VMEM,
         compiler_params=params(20),
         cost_estimate=hint(2),
         name="own_part",
-    )(hidden, down_vmem).astype(F32)
-    for part in received:
-        summed = summed + part.astype(F32)
-    returned = exchange(summed.astype(BF16).reshape(holders, SEND, features))
+    )(hidden, down_vmem)
+    summed = pl.pallas_call(
+        sum_kernel,
+        out_shape=shape(sent, BF16),
+        in_specs=[VMEM] * width,
+        out_specs=VMEM,
+        compiler_params=params(8),
+        name="sum",
+    )(part, *received)
+    returned = exchange(summed)
     return pl.pallas_call(
-        combine_kernel,
+        functools.partial(combine_kernel, pieces),
         out_shape=shape((rows, features), BF16),
         in_specs=[VMEM] * 2,
-        out_specs=VMEM,
+        out_specs=HBM,
+        scratch_shapes=[pltpu.VMEM((rows, features), BF16), pltpu.SemaphoreType.DMA((pieces,))],
         compiler_params=params(8),
         name="combine",
     )(coeff, returned)

time: 37.2 us -> 35.2 us (0.946)
  blocking collectives: 29.2 us -> 27.2 us
  starting transfers between devices: 0.17 us -> 0.76 us
    all_to_all x2, blocking collectives: 29.2 us -> 27.2 us  [exchange(): return lax.all_to_all(x, axes, split_axis=0, concat_axis=0, tiled=True)]
    ppermute x2, starting transfers between devices: 0.17 us -> 0.76 us  [shifted(): lax.ppermute(x, 'width', [(i, (i + d) % width) for i in range(width)])]
    pallas_call x5 -> x6, Pallas kernels: 5.66 us -> 5.71 us  [the longest x1 2.15 us: body(): pl.pallas_call(functools.partial(others_kernel, width - 1, pieces), out_s...]
  transfers between devices with their start and end apart: 2 -> 2, of which waited for: 2 -> 1; matrix products, arithmetic and copies ran while one was open for 0% -> 0% of each run, Pallas kernels for 6% -> 6%
where the time goes in v3:
time: 35.2 us; the launch traced here: 35 us
  blocking collectives  27.2 us (77%)
  Pallas kernels  6.76 us (19%)
  starting transfers between devices  0.76 us (2%)
    all_to_all x2, blocking collectives, exchange(): return lax.all_to_all(x, axes, split_axis=0, concat_axis=0, tiled=True)  27.2 us
    pallas_call x1, Pallas kernels, body(): pl.pallas_call(functools.partial(others_kernel, width - 1, pieces), out_s...  2.15 us
    pallas_call x1, Pallas kernels, body(): pl.pallas_call(functools.partial(own_kernel, pieces), out_shape=[shape((s...  1.18 us
    pallas_call x1, Pallas kernels, body(): pl.pallas_call(functools.partial(combine_kernel, pieces), out_shape=shape...  1.09 us
    pallas_call x1, Pallas kernels, body(): pl.pallas_call(slots_kernel, out_shape=(shape((slots, rows), BF16), shape...  1.05 us
    pallas_call x1, Pallas kernels, body(): pl.pallas_call(functools.partial(own_part_kernel, pieces), out_shape=shap...  1.01 us
    ppermute x2, starting transfers between devices, shifted(): lax.ppermute(x, 'width', [(i, (i + d) % width) for i in range(width)])  0.76 us
  transfers between devices with their start and end apart: 2, of which 1 were waited for; matrix products, arithmetic and copies ran while one was open for 0% of the time, Pallas kernels for 6%

profile of v3, /device:TPU:0, one launch (start us, length us, event | category | flops | bytes accessed | tf_op | source)
XLA Modules:
  0.0 35.0 jit_solution(4469438050084088146)
XLA Ops:
  0.0 1.1 %slots.1 = (bf16[32,64]{1,0:T(8,128)(2,1)S(1)}, f32[32,64]{1,0:T(8,128)S(1)}, bf16[64,3072]{1,0:T(8,128)(2,1)S(1)}) custom-call(s32[8,64]{1,0:T(8,128)} %bitcast.2, f32[8,64]{1,0:T(8,128)} %bitcast.3, bf16[64,3072]{1,0:T(8,128)(2,1)} %tokens_hbm.1), custom_call_target="tpu_custom_call" | custom-call | tf_op jit(solution)/shard_map/slots/pallas_call | solution.py:167
  1.1 0.0 copy-start
  1.1 0.0 copy-start.1
  1.1 0.0 copy-start.2
  1.1 0.2 select.1
  1.3 16.1 %all_to_all.10.rows_ref = bf16[32,2,1536]{2,1,0:T(2,128)(2,1)S(1)} all-to-all(bf16[32,2,1536]{2,1,0:T(2,128)(2,1)S(1)} %select.1), channel_id=1, replica_groups=mesh['expert'=16,'width'=2] {'expert','width'}, dimensions={0} | all-to-all | bytes 393216 | tf_op jit(solution)/shard_map/all_to_all | solution.py:196
  17.4 0.5 %collective-permute-start = (bf16[32,2,1536]{2,1,0:T(2,128)(2,1)S(1)}, bf16[32,2,1536]{2,1,0:T(2,128)(2,1)S(1)}, u32[]{:S(2)}, u32[]{:S(2)}) collective-permute-start(bf16[32,2,1536]{2,1,0:T(2,128)(2,1)S(1)} %all_to_all.10.rows_ref), channel_id=1, source_target_pairs={{0,1},{1,0},{2,3},{3,2},{4,5},{5,4},{6,7},{7,6},{8,9},{9,8},{10,11... | collective-permute-start | bytes 589832 | tf_op jit(solution)/shard_map/ppermute | solution.py:199
  17.9 0.0 copy-done
  17.9 0.0 copy-done.1
  17.9 0.0 copy-done.2
  17.9 1.2 %own.1 = (f32[32,512]{1,0:T(8,128)S(1)}, f32[32,512]{1,0:T(8,128)S(1)}) custom-call(bf16[32,2,1536]{2,1,0:T(2,128)(2,1)S(1)} %all_to_all.10.rows_ref, bf16[1,6144,512]{2,1,0:T(8,128)(2,1)S(1)} %copy-done, bf16[1,6144,512]{2,1,0:T(8,128)(2,1)S(1)} %copy-done.1, bf16[1,6144,512]{2,1,0:T(8,128)(2,1)S(1)} %copy-done.2), custom_call_target="tpu_custom_call" | custom-call | flops 2000000000 | tf_op jit(solution)/shard_map/own/pallas_call | solution.py:207
  19.1 0.0 collective-permute-done.refs_0_
  19.1 2.2 %others.1 = (bf16[32,512]{1,0:T(8,128)(2,1)S(1)}, bf16[32,3072]{1,0:T(8,128)(2,1)S(1)}) custom-call(bf16[32,2,1536]{2,1,0:T(2,128)(2,1)S(1)} %collective-permute-done.refs_0_, f32[32,512]{1,0:T(8,128)S(1)} %get-tuple-element.15.refs_1_, f32[32,512]{1,0:T(8,128)S(1)} %get-tuple-element.16.refs_2_, bf16[1,6144,512]{2,1,0:T(8,128)(2,1)S(1)} %copy-done, ...), custom_call_target="tpu_custom_call" | custom-call | flops 2000000000 | tf_op jit(solution)/shard_map/others/pallas_call | solution.py:216
  21.2 0.2 collective-permute-start.1
  21.5 1.0 %own_part.1.refs_0_ = bf16[32,3072]{1,0:T(8,128)(2,1)S(1)} custom-call(bf16[32,512]{1,0:T(8,128)(2,1)S(1)} %get-tuple-element.17.hidden_ref, bf16[1,6144,512]{2,1,0:T(8,128)(2,1)S(1)} %copy-done.2), custom_call_target="tpu_custom_call" | custom-call | flops 2000000000 | tf_op jit(solution)/shard_map/own_part/pallas_call | solution.py:227
  22.5 0.2 collective-permute-done.1.refs_1_
  22.7 0.1 sum.1
  22.8 11.1 %all_to_all.11.returned_ref = bf16[32,2,1536]{2,1,0:T(2,128)(2,1)S(1)} all-to-all(bf16[32,2,1536]{2,1,0:T(2,128)(2,1)S(1)} %sum.1), channel_id=1, replica_groups=mesh['expert'=16,'width'=2] {'expert','width'}, dimensions={0} | all-to-all | bytes 393216 | tf_op jit(solution)/shard_map/all_to_all | solution.py:196
  33.9 1.1 %combine.1 = bf16[64,3072]{1,0:T(8,128)(2,1)} custom-call(f32[32,64]{1,0:T(8,128)S(1)} %get-tuple-element.12.coeff_ref, bf16[32,2,1536]{2,1,0:T(2,128)(2,1)S(1)} %all_to_all.11.returned_ref), custom_call_target="tpu_custom_call" | custom-call | tf_op jit(solution)/shard_map/combine/pallas_call | solution.py:245
Async XLA Ops:
  1.1 16.8 %copy-start = (bf16[1,6144,512]{2,1,0:T(8,128)(2,1)S(1)}, bf16[1,6144,512]{2,1,0:T(8,128)(2,1)}, u32[]{:S(2)}) copy-start(bf16[1,6144,512]{2,1,0:T(8,128)(2,1)} %refs_3_.1) | copy-start | bytes 18874372
  1.1 16.8 %copy-start.1 = (bf16[1,6144,512]{2,1,0:T(8,128)(2,1)S(1)}, bf16[1,6144,512]{2,1,0:T(8,128)(2,1)}, u32[]{:S(2)}) copy-start(bf16[1,6144,512]{2,1,0:T(8,128)(2,1)} %refs_4_.1) | copy-start | bytes 18874372
  1.1 16.8 %copy-start.2 = (bf16[1,6144,512]{2,1,0:T(8,128)(2,1)S(1)}, bf16[1,6144,512]{2,1,0:T(8,128)(2,1)}, u32[]{:S(2)}) copy-start(bf16[1,6144,512]{2,1,0:T(8,128)(2,1)} %down_ref.3) | copy-start | bytes 18874372
  17.4 1.7 %collective-permute-start = (bf16[32,2,1536]{2,1,0:T(2,128)(2,1)S(1)}, bf16[32,2,1536]{2,1,0:T(2,128)(2,1)S(1)}, u32[]{:S(2)}, u32[]{:S(2)}) collective-permute-start(bf16[32,2,1536]{2,1,0:T(2,128)(2,1)S(1)} %all_to_all.10.rows_ref), channel_id=1, source_target_pairs={{0,1},{1,0},{2,3},{3,2},{4,5},{5,4},{6,7},{7,6},{8,9},{9,8},{10,11... | collective-permute-start | bytes 589832 | tf_op jit(solution)/shard_map/ppermute | solution.py:199
  21.2 1.5 %collective-permute-start.1 = (bf16[32,3072]{1,0:T(8,128)(2,1)S(1)}, bf16[32,3072]{1,0:T(8,128)(2,1)S(1)}, u32[]{:S(2)}, u32[]{:S(2)}) collective-permute-start(bf16[32,3072]{1,0:T(8,128)(2,1)S(1)} %get-tuple-element.18), channel_id=1, source_target_pairs={{0,1},{1,0},{2,3},{3,2},{4,5},{5,4},{6,7},{7,6},{8,9},{9,8},{10,11... | collective-permute-start | bytes 589832 | tf_op jit(solution)/shard_map/ppermute | solution.py:199

commit v4 on v3

--- a/solution.py
+++ b/solution.py
@@ -9,6 +9,7 @@
 
 SEND = 2
 LANES = 128
+STEPS = (512, 384, 256, 128)
 VMEM = pl.BlockSpec(memory_space=pltpu.VMEM)
 HBM = pl.BlockSpec(memory_space=pltpu.HBM)
 F32 = jnp.float32
@@ -91,9 +92,32 @@
     return gate, up
 
 
-def own_kernel(pieces, rows_ref, gate_ref, up_ref, down_ref, gate_out, up_out):
-    del down_ref
-    gate_out[...], up_out[...] = gate_up(rows_ref, gate_ref, up_ref, 0, pieces, 0.0, 0.0)
+def own_kernel(others, pieces, rows_ref, coeff_ref, gate_ref, up_ref, down_ref, *outs):
+    gate_out, up_out, split_ref = outs[:3]
+    turned = outs[3:]
+    coeff = coeff_ref[...].T
+    high = coeff.astype(BF16)
+    rows = coeff.shape[0]
+    split_ref[:rows, :] = high
+    split_ref[rows:, :] = (coeff - high.astype(F32)).astype(BF16)
+    piece = rows_ref.shape[2]
+    features = piece * pieces
+    step = next((n for n in STEPS if piece % n == 0), piece)
+    own = owned(0, features, pieces)
+    theirs = [owned(d + 1, features, pieces) for d in range(others)]
+    gate = up = 0.0
+    for u in range(pieces):
+        x = join_rows(rows_ref, u, pieces)
+        for i in range(0, piece, step):
+            block = pl.ds(pl.multiple_of(own[u].start + i, step), step)
+            gate += jnp.dot(x[:, i : i + step], gate_ref[0, block, :], preferred_element_type=F32)
+            up += jnp.dot(x[:, i : i + step], up_ref[0, block, :], preferred_element_type=F32)
+            at = u * piece + i
+            for d in range(others):
+                block = pl.ds(pl.multiple_of(theirs[d][u].start + i, step), step)
+                turned[d][:, at : at + step] = down_ref[0, block, :].T
+    gate_out[...] = gate
+    up_out[...] = up
 
 
 def down_part(hidden, down_ref, d, pieces, part_ref):
@@ -107,16 +131,16 @@
 
 def others_kernel(others, pieces, *refs):
     rows = refs[:others]
-    gate_in, up_in, gate_ref, up_ref, down_ref = refs[others : others + 5]
-    hidden_ref = refs[others + 5]
-    parts = refs[others + 6 :]
+    turned = refs[others : 2 * others]
+    gate_in, up_in, gate_ref, up_ref, hidden_ref = refs[2 * others : 2 * others + 5]
+    parts = refs[2 * others + 5 :]
     gate, up = gate_in[...], up_in[...]
     for d in range(others):
         gate, up = gate_up(rows[d], gate_ref, up_ref, d + 1, pieces, gate, up)
     hidden = (gate / (1.0 + jnp.exp(-gate)) * up).astype(BF16)
     hidden_ref[...] = hidden
     for d in range(others):
-        down_part(hidden, down_ref, d + 1, pieces, parts[d])
+        parts[d][...] = jnp.dot(hidden, turned[d][...], preferred_element_type=F32).astype(BF16)
 
 
 def own_part_kernel(pieces, hidden_ref, down_ref, part_ref):
@@ -132,18 +156,14 @@
 
 def combine_kernel(pieces, coeff_ref, returned_ref, mixed_hbm, mixed_ref, sems):
     coeff = coeff_ref[...]
-    high = coeff.astype(BF16)
-    low = (coeff - high.astype(F32)).astype(BF16)
-    dims = (((0,), (0,)), ((), ()))
+    rows = mixed_ref.shape[0]
     piece = returned_ref.shape[2]
     copies = []
     for u in range(pieces):
         returned = join_rows(returned_ref, u, pieces)
         block = (slice(None), pl.ds(u * piece, piece))
-        mixed_ref[block] = (
-            lax.dot_general(high, returned, dims, preferred_element_type=F32)
-            + lax.dot_general(low, returned, dims, preferred_element_type=F32)
-        ).astype(BF16)
+        mixed = jnp.dot(coeff, returned, preferred_element_type=F32)
+        mixed_ref[block] = (mixed[:rows] + mixed[rows:]).astype(BF16)
         copies.append(pltpu.make_async_copy(mixed_ref.at[block], mixed_hbm.at[block], sems.at[u]))
         copies[-1].start()
     for copy in copies:
@@ -204,25 +224,27 @@
         pltpu.with_memory_space_constraint(w, pltpu.VMEM)
         for w in (gate_weight, up_weight, down_weight)
     )
-    gate, up = pl.pallas_call(
-        functools.partial(own_kernel, pieces),
-        out_shape=[shape((slots, hidden_units), F32)] * 2,
-        in_specs=[VMEM] * 4,
-        out_specs=[VMEM] * 2,
+    gate, up, coeff, *turned = pl.pallas_call(
+        functools.partial(own_kernel, width - 1, pieces),
+        out_shape=[shape((slots, hidden_units), F32)] * 2
+        + [shape((2 * rows, slots), BF16)]
+        + [shape((hidden_units, features), BF16)] * (width - 1),
+        in_specs=[VMEM] * 5,
+        out_specs=[VMEM] * (width + 2),
         compiler_params=params(20),
         cost_estimate=hint(2),
         name="own",
-    )(arrived, gate_vmem, up_vmem, down_vmem)
+    )(arrived, coeff, gate_vmem, up_vmem, down_vmem)
     hidden, *parts = pl.pallas_call(
         functools.partial(others_kernel, width - 1, pieces),
         out_shape=[shape((slots, hidden_units), BF16)]
         + [shape((slots, features), BF16)] * (width - 1),
-        in_specs=[VMEM] * (width + 4),
+        in_specs=[VMEM] * (2 * width + 2),
         out_specs=[VMEM] * width,
         compiler_params=params(24),
         cost_estimate=hint(2),
         name="others",
-    )(*others, gate, up, gate_vmem, up_vmem, down_vmem)
+    )(*others, *turned, gate, up, gate_vmem, up_vmem)
     received = [shifted(part, d + 1) for d, part in enumerate(reversed(parts))]
     part = pl.pallas_call(
         functools.partial(own_part_kernel, pieces),

time: 35.2 us -> 34.8 us (0.989)
    pallas_call x1, Pallas kernels: 2.15 us -> 1.8 us  [body(): pl.pallas_call(functools.partial(others_kernel, width - 1, pieces), out_s...]
where the time goes in v4:
time: 34.8 us; the launch traced here: 34.6 us
  blocking collectives  27.1 us (78%)
  Pallas kernels  6.42 us (18%)
  starting transfers between devices  0.72 us (2%)
    all_to_all x2, blocking collectives, exchange(): return lax.all_to_all(x, axes, split_axis=0, concat_axis=0, tiled=True)  27.1 us
    pallas_call x1, Pallas kernels, body(): pl.pallas_call(functools.partial(others_kernel, width - 1, pieces), out_s...  1.8 us
    pallas_call x1, Pallas kernels, body(): pl.pallas_call(functools.partial(own_kernel, width - 1, pieces), out_shap...  1.22 us
    pallas_call x1, Pallas kernels, body(): pl.pallas_call(functools.partial(combine_kernel, pieces), out_shape=shape...  1.06 us
    pallas_call x1, Pallas kernels, body(): pl.pallas_call(slots_kernel, out_shape=(shape((slots, rows), BF16), shape...  1.05 us
    pallas_call x1, Pallas kernels, body(): pl.pallas_call(functools.partial(own_part_kernel, pieces), out_shape=shap...  1.01 us
    ppermute x2, starting transfers between devices, shifted(): lax.ppermute(x, 'width', [(i, (i + d) % width) for i in range(width)])  0.72 us
  transfers between devices with their start and end apart: 2, of which 1 were waited for; matrix products, arithmetic and copies ran while one was open for 0% of the time, Pallas kernels for 6%

profile of v4, /device:TPU:0, one launch (start us, length us, event | category | flops | bytes accessed | tf_op | source)
XLA Modules:
  0.0 34.6 jit_solution(16666836461890796957)
XLA Ops:
  0.0 1.1 %slots.1 = (bf16[32,64]{1,0:T(8,128)(2,1)S(1)}, f32[32,64]{1,0:T(8,128)S(1)}, bf16[64,3072]{1,0:T(8,128)(2,1)S(1)}) custom-call(s32[8,64]{1,0:T(8,128)} %bitcast.2, f32[8,64]{1,0:T(8,128)} %bitcast.3, bf16[64,3072]{1,0:T(8,128)(2,1)} %tokens_hbm.1), custom_call_target="tpu_custom_call" | custom-call | tf_op jit(solution)/shard_map/slots/pallas_call | solution.py:187
  1.1 0.0 copy-start
  1.1 0.0 copy-start.1
  1.1 0.0 copy-start.2
  1.1 0.2 select.1
  1.3 16.1 %all_to_all.10.rows_ref = bf16[32,2,1536]{2,1,0:T(2,128)(2,1)S(1)} all-to-all(bf16[32,2,1536]{2,1,0:T(2,128)(2,1)S(1)} %select.1), channel_id=1, replica_groups=mesh['expert'=16,'width'=2] {'expert','width'}, dimensions={0} | all-to-all | bytes 393216 | tf_op jit(solution)/shard_map/all_to_all | solution.py:216
  17.4 0.5 %collective-permute-start = (bf16[32,2,1536]{2,1,0:T(2,128)(2,1)S(1)}, bf16[32,2,1536]{2,1,0:T(2,128)(2,1)S(1)}, u32[]{:S(2)}, u32[]{:S(2)}) collective-permute-start(bf16[32,2,1536]{2,1,0:T(2,128)(2,1)S(1)} %all_to_all.10.rows_ref), channel_id=1, source_target_pairs={{0,1},{1,0},{2,3},{3,2},{4,5},{5,4},{6,7},{7,6},{8,9},{9,8},{10,11... | collective-permute-start | bytes 589832 | tf_op jit(solution)/shard_map/ppermute | solution.py:219
  17.9 0.0 copy-done
  17.9 0.0 copy-done.1
  17.9 0.0 copy-done.2
  17.9 1.2 %own.1 = (f32[32,512]{1,0:T(8,128)S(1)}, f32[32,512]{1,0:T(8,128)S(1)}, bf16[128,32]{1,0:T(8,128)(2,1)S(1)}, bf16[512,3072]{1,0:T(8,128)(2,1)S(1)}) custom-call(bf16[32,2,1536]{2,1,0:T(2,128)(2,1)S(1)} %all_to_all.10.rows_ref, f32[32,64]{1,0:T(8,128)S(1)} %get-tuple-element.16.coeff_ref, bf16[1,6144,512]{2,1,0:T(8,128)(2,1)S(1)} %copy-done, ...), custom_call_target="tpu_custom_call" | custom-call | flops 2000000000 | tf_op jit(solution)/shard_map/own/pallas_call | solution.py:227
  19.1 0.0 collective-permute-done.refs_0_
  19.1 1.8 %others.1 = (bf16[32,512]{1,0:T(8,128)(2,1)S(1)}, bf16[32,3072]{1,0:T(8,128)(2,1)S(1)}) custom-call(bf16[32,2,1536]{2,1,0:T(2,128)(2,1)S(1)} %collective-permute-done.refs_0_, bf16[512,3072]{1,0:T(8,128)(2,1)S(1)} %get-tuple-element.18.refs_1_, f32[32,512]{1,0:T(8,128)S(1)} %get-tuple-element.19.refs_2_, f32[32,512]{1,0:T(8,128)S(1)} %get-tuple-element.20.refs_3_, ...), custom_call_target="tpu_custom_call" | custom-call | flops 2000000000 | tf_op jit(solution)/shard_map/others/pallas_call | solution.py:238
  20.9 0.2 collective-permute-start.1
  21.1 1.0 %own_part.1.refs_0_ = bf16[32,3072]{1,0:T(8,128)(2,1)S(1)} custom-call(bf16[32,512]{1,0:T(8,128)(2,1)S(1)} %get-tuple-element.21.hidden_ref, bf16[1,6144,512]{2,1,0:T(8,128)(2,1)S(1)} %copy-done.2), custom_call_target="tpu_custom_call" | custom-call | flops 2000000000 | tf_op jit(solution)/shard_map/own_part/pallas_call | solution.py:249
  22.2 0.2 collective-permute-done.1.refs_1_
  22.4 0.1 sum.1
  22.5 11.1 %all_to_all.11.returned_ref = bf16[32,2,1536]{2,1,0:T(2,128)(2,1)S(1)} all-to-all(bf16[32,2,1536]{2,1,0:T(2,128)(2,1)S(1)} %sum.1), channel_id=1, replica_groups=mesh['expert'=16,'width'=2] {'expert','width'}, dimensions={0} | all-to-all | bytes 393216 | tf_op jit(solution)/shard_map/all_to_all | solution.py:216
  33.5 1.1 %combine.1 = bf16[64,3072]{1,0:T(8,128)(2,1)} custom-call(bf16[128,32]{1,0:T(8,128)(2,1)S(1)} %get-tuple-element.17.coeff_ref, bf16[32,2,1536]{2,1,0:T(2,128)(2,1)S(1)} %all_to_all.11.returned_ref), custom_call_target="tpu_custom_call" | custom-call | tf_op jit(solution)/shard_map/combine/pallas_call | solution.py:267
Async XLA Ops:
  1.1 16.8 %copy-start = (bf16[1,6144,512]{2,1,0:T(8,128)(2,1)S(1)}, bf16[1,6144,512]{2,1,0:T(8,128)(2,1)}, u32[]{:S(2)}) copy-start(bf16[1,6144,512]{2,1,0:T(8,128)(2,1)} %refs_4_.1) | copy-start | bytes 18874372
  1.1 16.8 %copy-start.1 = (bf16[1,6144,512]{2,1,0:T(8,128)(2,1)S(1)}, bf16[1,6144,512]{2,1,0:T(8,128)(2,1)}, u32[]{:S(2)}) copy-start(bf16[1,6144,512]{2,1,0:T(8,128)(2,1)} %refs_5_.1) | copy-start | bytes 18874372
  1.1 16.8 %copy-start.2 = (bf16[1,6144,512]{2,1,0:T(8,128)(2,1)S(1)}, bf16[1,6144,512]{2,1,0:T(8,128)(2,1)}, u32[]{:S(2)}) copy-start(bf16[1,6144,512]{2,1,0:T(8,128)(2,1)} %down_ref.3) | copy-start | bytes 18874372
  17.4 1.7 %collective-permute-start = (bf16[32,2,1536]{2,1,0:T(2,128)(2,1)S(1)}, bf16[32,2,1536]{2,1,0:T(2,128)(2,1)S(1)}, u32[]{:S(2)}, u32[]{:S(2)}) collective-permute-start(bf16[32,2,1536]{2,1,0:T(2,128)(2,1)S(1)} %all_to_all.10.rows_ref), channel_id=1, source_target_pairs={{0,1},{1,0},{2,3},{3,2},{4,5},{5,4},{6,7},{7,6},{8,9},{9,8},{10,11... | collective-permute-start | bytes 589832 | tf_op jit(solution)/shard_map/ppermute | solution.py:219
  20.9 1.5 %collective-permute-start.1 = (bf16[32,3072]{1,0:T(8,128)(2,1)S(1)}, bf16[32,3072]{1,0:T(8,128)(2,1)S(1)}, u32[]{:S(2)}, u32[]{:S(2)}) collective-permute-start(bf16[32,3072]{1,0:T(8,128)(2,1)S(1)} %get-tuple-element.22), channel_id=1, source_target_pairs={{0,1},{1,0},{2,3},{3,2},{4,5},{5,4},{6,7},{7,6},{8,9},{9,8},{10,11... | collective-permute-start | bytes 589832 | tf_op jit(solution)/shard_map/ppermute | solution.py:219
